TPU v7x, 32 devices: a whole 2x2x4 slice. The times are simulated.
32 devices in a mesh: grp: 4 (over x, core), clu: 8 (over z, y).
Axes of the slice: x: 2, y: 2, z: 4, core: 2. Of those that a mesh axis runs over, the one named last changes fastest.
Arguments:
- radiosity: float32 [128, 3, 128], P(('grp', 'clu')), may hold values from 0 to 3
- form_factors: float32 [4096, 128, 128], P(('grp', 'clu')), may hold values from 0.01 to 16
- source_device: int32 [4096, 1], P(('grp', 'clu')), may hold values from 0 to 31; in each aligned block of 128 rows (0 to 127, 128 to 255, ...) at most 8 rows name the same one
- source_slot: int32 [4096], P(('grp', 'clu')), may hold values from 0 to 3
- receiver_slot: int32 [4096], P(('grp', 'clu')), may hold values from 0 to 3
- emission: float32 [128, 3, 128], P(('grp', 'clu')), may hold values from 0.1 to 2
- reflectance: float32 [128, 3, 128], P(('grp', 'clu')), may hold values from 0.3 to 0.9
- patch_area: float32 [128, 128], P(('grp', 'clu')), may hold values from 0.5 to 2
- cluster_group: int32 [128], P(('grp', 'clu')), may hold values from 0 to 15, as said below
- group_coupling: float32 [16, 16], replicated, may hold values from 0 to 1
- ambient: float32 [3], replicated, may hold values from 0.2 to 1
Outputs:
- radiosity_new: float32 [128, 3, 128], P(('grp', 'clu'))
- group_radiosity: float32 [16, 3], replicated
Inputs may be any that keep to these rules, and one draw needn't show every extreme that they name: `source_device`: the rows of one device name each source device at most 8 times. `cluster_group`: each group node has exactly 8 clusters.
All inputs are finite; a program needn't handle non-finite values.
Results may differ from a plain program's by a relative error of at most 0.00005.
Values sent between devices are 32-bit elements; how exact they have to be, the bound alone decides.
No kernel may reach another device: no remote copies, remote signals or barrier semaphores. Data moves between devices by JAX's collectives and lax.ppermute only.
A program may use at most 64 MiB of HBM per device.

v0:
```python
import jax
import jax.numpy as jnp
from jax import lax
from jax.sharding import PartitionSpec as P


def cluster_sums(field, patch_area):
    return jnp.einsum("kci,ki->kc", field, patch_area, precision=lax.Precision.HIGHEST)


def on_device(
    radiosity,
    form_factors,
    source_device,
    source_slot,
    receiver_slot,
    emission,
    reflectance,
    patch_area,
    cluster_group,
    group_coupling,
    ambient,
):
    clusters_here = radiosity.shape[0]
    count = form_factors.shape[0]
    width = form_factors.shape[1]
    groups_all = group_coupling.shape[0]
    devices = lax.axis_size("grp") * lax.axis_size("clu")
    scale = 2.0 * clusters_here / (width * count)
    sources = source_device[:, 0]
    capacity = max(2, 2 * count // devices)
    order = jnp.arange(count, dtype=jnp.int32)
    earlier = (sources[None, :] == sources[:, None]) & (order[None, :] < order[:, None])
    ranking = jnp.sum(earlier.astype(jnp.int32), axis=1)
    position = sources * capacity + ranking
    wanted = jnp.zeros((devices * capacity,), jnp.int32).at[position].set(source_slot + 1)
    asked = lax.all_to_all(
        wanted.reshape(devices, capacity), ("grp", "clu"), split_axis=0, concat_axis=0, tiled=True
    ).reshape(devices * capacity)
    valid = (asked > 0).astype(jnp.float32)
    answer = jnp.take(radiosity, jnp.maximum(asked - 1, 0), axis=0) * valid[:, None, None]
    returned = lax.all_to_all(
        answer.reshape(devices, capacity, 3, width),
        ("grp", "clu"),
        split_axis=0,
        concat_axis=0,
        tiled=True,
    ).reshape(devices * capacity, 3, width)
    fetched = jnp.take(returned, position, axis=0)
    contribution = (
        jnp.einsum("lij,lcj->lci", form_factors, fetched, precision=lax.Precision.HIGHEST) * scale
    )
    receiver_table = (
        receiver_slot[:, None] == jnp.arange(clusters_here, dtype=jnp.int32)[None, :]
    ).astype(jnp.float32)
    irradiance = jnp.einsum(
        "lk,lci->kci", receiver_table, contribution, precision=lax.Precision.HIGHEST
    )
    group_table = (
        cluster_group[:, None] == jnp.arange(groups_all, dtype=jnp.int32)[None, :]
    ).astype(jnp.float32)
    local_sum = jnp.dot(
        group_table.T, cluster_sums(radiosity, patch_area), precision=lax.Precision.HIGHEST
    )
    local_area = jnp.dot(
        group_table.T, jnp.sum(patch_area, axis=1), precision=lax.Precision.HIGHEST
    )
    group_sum, group_area = lax.psum((local_sum, local_area), ("grp", "clu"))
    old_group = group_sum / group_area[:, None]
    old_root = jnp.sum(group_sum, axis=0) / jnp.sum(group_area)
    group_irradiance = jnp.dot(
        group_coupling / groups_all, old_group, precision=lax.Precision.HIGHEST
    )
    coarse = (
        jnp.dot(group_table, group_irradiance, precision=lax.Precision.HIGHEST)
        + (ambient * old_root)[None, :]
    )
    radiosity_new = emission + reflectance * (irradiance + coarse[:, :, None])
    new_local = jnp.dot(
        group_table.T, cluster_sums(radiosity_new, patch_area), precision=lax.Precision.HIGHEST
    )
    new_sum = lax.psum(new_local, ("grp", "clu"))
    return (radiosity_new, new_sum / group_area[:, None])


def solution(mesh):
    return jax.shard_map(
        on_device,
        mesh=mesh,
        in_specs=(
            P(("grp", "clu"), None, None),
            P(("grp", "clu"), None, None),
            P(("grp", "clu"), None),
            P(("grp", "clu")),
            P(("grp", "clu")),
            P(("grp", "clu"), None, None),
            P(("grp", "clu"), None, None),
            P(("grp", "clu"), None),
            P(("grp", "clu")),
            P(),
            P(),
        ),
        out_specs=(P(("grp", "clu"), None, None), P()),
        check_vma=False,
    )
```

profile of v0, /device:TPU:0, one launch (start us, length us, event | category | flops | bytes accessed | tf_op | source)
XLA Modules:
  0.0 133.1 jit_solution(4761366920443387148)
XLA Ops:
  0.6 0.9 convert_reduce_fusion
  1.6 0.7 and_bitcast_fusion
  2.2 0.7 broadcast_add_fusion
  2.9 1.0 scatter_custom_fusion
  3.9 0.7 all_to_all.9
  4.5 7.3 %all-to-all-start = ((s32[32,1,8]{2,1,0:T(1,128)}), s32[32,1,8]{2,1,0:T(1,128)S(1)}, u32[]{:S(2)}, u32[]{:S(2)}) async-start(s32[32,1,8]{2,1,0:T(1,128)} %bitcast.5), calls=%async_computation | async-start | bytes 32768 | tf_op jit(solution)/shard_map/all_to_all | solution.py:37
  12.0 0.8 fusion.12
  12.9 0.9 fusion.18
  13.7 0.8 convolution_bitcast_fusion
  14.5 40.4 %all-reduce = (f32[16,3]{0,1:T(4,128)S(1)}, f32[16]{0:T(128)S(1)}) all-reduce(f32[16,3]{0,1:T(4,128)S(1)} %fusion.18, f32[16]{0:T(128)S(1)} %convolution_bitcast_fusion), channel_id=1, replica_groups=mesh['grp'=4,'clu'=8] {'grp','clu'}, use_global_device_ids=true, to_apply=%region_2.3 | all-reduce | flops 64 | bytes 512 | tf_op jit(solution)/shard_map/psum | solution.py:68
  54.9 0.6 reduce_sum.42
  56.1 2.1 %gather_fusion = f32[256,3,128]{2,0,1:T(8,128)S(1)} fusion(f32[4,3,128]{2,0,1:T(4,128)} %param.11, s32[1024]{0:T(1024)S(1)} %pad_clamp_fusion.1), kind=kCustom, calls=%fused_computation | custom fusion | bytes 787456 | tf_op jit(solution)/shard_map/jit(_take)/gather | solution.py:41
  58.2 0.9 fusion.2
  59.1 4.5 %all-to-all-start.1 = ((f32[32,8,3,128]{3,1,2,0:T(8,128)}), f32[32,8,3,128]{3,1,2,0:T(8,128)S(1)}, u32[]{:S(2)}, u32[]{:S(2)}) async-start(f32[32,8,3,128]{3,1,2,0:T(8,128)} %fusion.2), calls=%async_computation.1 | async-start | bytes 786432 | tf_op jit(solution)/shard_map/all_to_all | solution.py:42
  63.6 1.3 divide_multiply_fusion
  64.9 0.8 fusion.8
  65.7 0.8 convolution_add_fusion.1
  66.6 10.4 %all-to-all-done.1 = f32[32,8,3,128]{3,1,2,0:T(8,128)S(1)} async-done(((f32[32,8,3,128]{3,1,2,0:T(8,128)}), f32[32,8,3,128]{3,1,2,0:T(8,128)S(1)}, u32[]{:S(2)}, u32[]{:S(2)}) %all-to-all-start.1) | async-done | bytes 393248 | tf_op jit(solution)/shard_map/all_to_all | solution.py:42
  77.2 0.8 gather_fusion.1
  77.9 15.5 %convolution_multiply_fusion = f32[128,3,128]{2,1,0:T(4,128)S(1)} fusion(f32[128,128,128]{2,1,0:T(8,128)} %param.12, f32[128,3,128]{2,1,0:T(4,128)S(1)} %gather_fusion.1, pred[128]{0:T(512)(128)(4,1)S(1)} %get-tuple-element.4), kind=kOutput, calls=%fused_computation.3 | convolution fusion | flops 75595776 | bytes 8781952 | tf_op jit(solution)/shard_map/lij,lcj->lci/dot_general | solution.py:51
  93.4 0.2 fusion.1
  93.8 0.2 fusion.17
  94.0 38.5 %psum.23 = f32[16,3]{0,1:T(4,128)S(1)} all-reduce(f32[16,3]{0,1:T(4,128)S(1)} %fusion.17), channel_id=1, replica_groups=mesh['grp'=4,'clu'=8] {'grp','clu'}, use_global_device_ids=true, to_apply=%region_7.8 | all-reduce | flops 48 | bytes 384 | tf_op jit(solution)/shard_map/psum | solution.py:82
  132.5 0.6 broadcast_divide_fusion
  (26 shorter events, 1.0 us)
Async XLA Ops:
  0.6 11.3 %copy-start = (f32[4,128]{1,0:T(4,128)S(1)}, f32[4,128]{1,0:T(4,128)}, u32[]{:S(2)}) copy-start(f32[4,128]{1,0:T(4,128)} %param.18) | copy-start | bytes 6148
  4.5 51.1 %all-to-all-start = ((s32[32,1,8]{2,1,0:T(1,128)}), s32[32,1,8]{2,1,0:T(1,128)S(1)}, u32[]{:S(2)}, u32[]{:S(2)}) async-start(s32[32,1,8]{2,1,0:T(1,128)} %bitcast.5), calls=%async_computation | async-start | bytes 32768 | tf_op jit(solution)/shard_map/all_to_all | solution.py:37
  56.1 37.3 %copy-start.1 = (f32[4,3,128]{2,0,1:T(4,128)S(1)}, f32[4,3,128]{2,0,1:T(4,128)}, u32[]{:S(2)}) copy-start(f32[4,3,128]{2,0,1:T(4,128)} %param.16) | copy-start | bytes 18436
  56.1 37.3 %copy-start.2 = (f32[4,3,128]{2,0,1:T(4,128)S(1)}, f32[4,3,128]{2,0,1:T(4,128)}, u32[]{:S(2)}) copy-start(f32[4,3,128]{2,0,1:T(4,128)} %param.17) | copy-start | bytes 18436
  56.1 37.3 %copy-start.4 = (s32[128]{0:T(128)S(1)}, s32[128]{0:T(128)}, u32[]{:S(2)}) copy-start(s32[128]{0:T(128)} %param.15) | copy-start | bytes 1540
  56.1 37.6 %copy-start.5 = (s32[4]{0:T(128)S(1)}, s32[4]{0:T(128)}, u32[]{:S(2)}) copy-start(s32[4]{0:T(128)} %param.19) | copy-start | bytes 52
  59.1 17.9 %all-to-all-start.1 = ((f32[32,8,3,128]{3,1,2,0:T(8,128)}), f32[32,8,3,128]{3,1,2,0:T(8,128)S(1)}, u32[]{:S(2)}, u32[]{:S(2)}) async-start(f32[32,8,3,128]{3,1,2,0:T(8,128)} %fusion.2), calls=%async_computation.1 | async-start | bytes 786432 | tf_op jit(solution)/shard_map/all_to_all | solution.py:42
  93.6 39.5 %copy-start.3 = (f32[4,3,128]{2,0,1:T(4,128)}, f32[4,3,128]{2,0,1:T(4,128)S(1)}, u32[]{:S(2)}) copy-start(f32[4,3,128]{2,0,1:T(4,128)S(1)} %fusion.1) | copy-start | bytes 18436
where the time goes:
time: 134 us; the launch traced here: 133 us
  blocking collectives  79 us (59%)
  matrix products  20.2 us (15%)
  starting transfers between devices  11.8 us (9%)
  waiting for transfers between devices  10.4 us (8%)
  other arithmetic  5.86 us (4%)
  local copies, waits for them, and re-layouts  5.07 us (4%)
    psum x1, blocking collectives, on_device(): group_sum, group_area = lax.psum((local_sum, local_area), ('grp', 'clu'))  40.4 us
    psum x1, blocking collectives, on_device(): new_sum = lax.psum(new_local, ('grp', 'clu'))  38.5 us
    dot_general x1, matrix products, on_device(): jnp.einsum('lij,lcj->lci', form_factors, fetched, precision=lax.Precision...  15.5 us
    all_to_all x1, waiting for transfers between devices, on_device(): lax.all_to_all(answer.reshape(devices, capacity, 3, width), ('grp', 'clu'...  10.4 us
    all_to_all x1, starting transfers between devices, on_device(): lax.all_to_all(wanted.reshape(devices, capacity), ('grp', 'clu'), split_a...  7.33 us
    all_to_all x1, starting transfers between devices, on_device(): lax.all_to_all(answer.reshape(devices, capacity, 3, width), ('grp', 'clu'...  4.48 us
  transfers between devices with their start and end apart: 2, of which 1 were waited for; matrix products, arithmetic and copies ran while one was open for 5% of the time, Pallas kernels for 0%

commit v1 on v0

--- a/solution.py
+++ b/solution.py
@@ -79,7 +79,7 @@
     new_local = jnp.dot(
         group_table.T, cluster_sums(radiosity_new, patch_area), precision=lax.Precision.HIGHEST
     )
-    new_sum = lax.psum(new_local, ("grp", "clu"))
+    new_sum = jnp.sum(jax.lax.all_gather(new_local, axis_name=("grp", "clu")), axis=0)
     return (radiosity_new, new_sum / group_area[:, None])
 
 

time: 134 us -> 160 us (1.19)
  blocking collectives: 79 us -> 105 us
    all_gather x0 -> x1, blocking collectives: none -> 64.8 us  [on_device(): jax.lax.all_gather(new_local, axis_name=('grp', 'clu'))]
    psum x1 -> x0, blocking collectives: 38.5 us -> none  [on_device(): new_sum = lax.psum(new_local, ('grp', 'clu'))]
  transfers between devices with their start and end apart: 2 -> 2, of which waited for: 1 -> 1; matrix products, arithmetic and copies ran while one was open for 5% -> 4% of each run, Pallas kernels for 0% -> 0%
where the time goes in v1:
time: 160 us; the launch traced here: 159 us
  blocking collectives  105 us (66%)
  matrix products  20.2 us (13%)
  starting transfers between devices  11.8 us (7%)
  waiting for transfers between devices  10.4 us (6%)
  other arithmetic  5.91 us (4%)
  local copies, waits for them, and re-layouts  5.07 us (3%)
    all_gather x1, blocking collectives, on_device(): jax.lax.all_gather(new_local, axis_name=('grp', 'clu'))  64.8 us
    psum x1, blocking collectives, on_device(): group_sum, group_area = lax.psum((local_sum, local_area), ('grp', 'clu'))  40.4 us
    dot_general x1, matrix products, on_device(): jnp.einsum('lij,lcj->lci', form_factors, fetched, precision=lax.Precision...  15.5 us
    all_to_all x1, waiting for transfers between devices, on_device(): lax.all_to_all(answer.reshape(devices, capacity, 3, width), ('grp', 'clu'...  10.4 us
    all_to_all x1, starting transfers between devices, on_device(): lax.all_to_all(wanted.reshape(devices, capacity), ('grp', 'clu'), split_a...  7.33 us
    all_to_all x1, starting transfers between devices, on_device(): lax.all_to_all(answer.reshape(devices, capacity, 3, width), ('grp', 'clu'...  4.48 us
  transfers between devices with their start and end apart: 2, of which 1 were waited for; matrix products, arithmetic and copies ran while one was open for 4% of the time, Pallas kernels for 0%

profile of v1, /device:TPU:0, one launch (start us, length us, event | category | flops | bytes accessed | tf_op | source)
XLA Modules:
  0.0 159.4 jit_solution(7445795342412630782)
XLA Ops:
  0.6 0.9 convert_reduce_fusion
  1.6 0.7 and_bitcast_fusion
  2.2 0.7 broadcast_add_fusion
  2.9 1.0 scatter_custom_fusion
  3.9 0.7 all_to_all.9
  4.5 7.3 %all-to-all-start = ((s32[32,1,8]{2,1,0:T(1,128)}), s32[32,1,8]{2,1,0:T(1,128)S(1)}, u32[]{:S(2)}, u32[]{:S(2)}) async-start(s32[32,1,8]{2,1,0:T(1,128)} %bitcast.5), calls=%async_computation | async-start | bytes 32768 | tf_op jit(solution)/shard_map/all_to_all | solution.py:37
  12.0 0.8 fusion.12
  12.9 0.9 fusion.17
  13.7 0.8 convolution_bitcast_fusion.1
  14.5 40.4 %all-reduce = (f32[16,3]{0,1:T(4,128)S(1)}, f32[16]{0:T(128)S(1)}) all-reduce(f32[16,3]{0,1:T(4,128)S(1)} %fusion.17, f32[16]{0:T(128)S(1)} %convolution_bitcast_fusion.1), channel_id=1, replica_groups=mesh['grp'=4,'clu'=8] {'grp','clu'}, use_global_device_ids=true, to_apply=%region_2.3 | all-reduce | flops 64 | bytes 512 | tf_op jit(solution)/shard_map/psum | solution.py:68
  54.9 0.6 reduce_sum.51
  56.1 2.1 %gather_fusion = f32[256,3,128]{2,0,1:T(8,128)S(1)} fusion(f32[4,3,128]{2,0,1:T(4,128)} %param.11, s32[1024]{0:T(1024)S(1)} %pad_clamp_fusion.1), kind=kCustom, calls=%fused_computation | custom fusion | bytes 787456 | tf_op jit(solution)/shard_map/jit(_take)/gather | solution.py:41
  58.2 0.9 fusion.2
  59.1 4.5 %all-to-all-start.1 = ((f32[32,8,3,128]{3,1,2,0:T(8,128)}), f32[32,8,3,128]{3,1,2,0:T(8,128)S(1)}, u32[]{:S(2)}, u32[]{:S(2)}) async-start(f32[32,8,3,128]{3,1,2,0:T(8,128)} %fusion.2), calls=%async_computation.1 | async-start | bytes 786432 | tf_op jit(solution)/shard_map/all_to_all | solution.py:42
  63.6 1.3 divide_multiply_fusion
  64.9 0.8 fusion.8
  65.7 0.8 convolution_add_fusion.1
  66.6 10.4 %all-to-all-done.1 = f32[32,8,3,128]{3,1,2,0:T(8,128)S(1)} async-done(((f32[32,8,3,128]{3,1,2,0:T(8,128)}), f32[32,8,3,128]{3,1,2,0:T(8,128)S(1)}, u32[]{:S(2)}, u32[]{:S(2)}) %all-to-all-start.1) | async-done | bytes 393248 | tf_op jit(solution)/shard_map/all_to_all | solution.py:42
  77.2 0.8 gather_fusion.1
  77.9 15.5 %convolution_multiply_fusion = f32[128,3,128]{2,1,0:T(4,128)S(1)} fusion(f32[128,128,128]{2,1,0:T(8,128)} %param.12, f32[128,3,128]{2,1,0:T(4,128)S(1)} %gather_fusion.1, pred[128]{0:T(512)(128)(4,1)S(1)} %get-tuple-element.4), kind=kOutput, calls=%fused_computation.3 | convolution fusion | flops 75595776 | bytes 8781952 | tf_op jit(solution)/shard_map/lij,lcj->lci/dot_general | solution.py:51
  93.4 0.2 fusion.1
  93.8 0.2 convolution_bitcast_fusion
  94.0 64.8 %all-gather.1 = f32[32,16,3]{1,2,0:T(4,128)S(1)} all-gather(f32[1,16,3]{1,2,0:T(4,128)S(1)} %convolution_bitcast_fusion), channel_id=2, replica_groups=mesh['grp'=4,'clu'=8] {'grp','clu'}, dimensions={0}, use_global_device_ids=true | all-gather | bytes 6336 | tf_op jit(solution)/shard_map/all_gather | solution.py:82
  158.8 0.6 broadcast_divide_fusion
  (27 shorter events, 1.0 us)
Async XLA Ops:
  0.6 11.3 %copy-start = (f32[4,128]{1,0:T(4,128)S(1)}, f32[4,128]{1,0:T(4,128)}, u32[]{:S(2)}) copy-start(f32[4,128]{1,0:T(4,128)} %param.18) | copy-start | bytes 6148
  4.5 51.1 %all-to-all-start = ((s32[32,1,8]{2,1,0:T(1,128)}), s32[32,1,8]{2,1,0:T(1,128)S(1)}, u32[]{:S(2)}, u32[]{:S(2)}) async-start(s32[32,1,8]{2,1,0:T(1,128)} %bitcast.5), calls=%async_computation | async-start | bytes 32768 | tf_op jit(solution)/shard_map/all_to_all | solution.py:37
  56.1 37.3 %copy-start.1 = (f32[4,3,128]{2,0,1:T(4,128)S(1)}, f32[4,3,128]{2,0,1:T(4,128)}, u32[]{:S(2)}) copy-start(f32[4,3,128]{2,0,1:T(4,128)} %param.16) | copy-start | bytes 18436
  56.1 37.3 %copy-start.2 = (f32[4,3,128]{2,0,1:T(4,128)S(1)}, f32[4,3,128]{2,0,1:T(4,128)}, u32[]{:S(2)}) copy-start(f32[4,3,128]{2,0,1:T(4,128)} %param.17) | copy-start | bytes 18436
  56.1 37.3 %copy-start.4 = (s32[128]{0:T(128)S(1)}, s32[128]{0:T(128)}, u32[]{:S(2)}) copy-start(s32[128]{0:T(128)} %param.15) | copy-start | bytes 1540
  56.1 37.6 %copy-start.5 = (s32[4]{0:T(128)S(1)}, s32[4]{0:T(128)}, u32[]{:S(2)}) copy-start(s32[4]{0:T(128)} %param.19) | copy-start | bytes 52
  59.1 17.9 %all-to-all-start.1 = ((f32[32,8,3,128]{3,1,2,0:T(8,128)}), f32[32,8,3,128]{3,1,2,0:T(8,128)S(1)}, u32[]{:S(2)}, u32[]{:S(2)}) async-start(f32[32,8,3,128]{3,1,2,0:T(8,128)} %fusion.2), calls=%async_computation.1 | async-start | bytes 786432 | tf_op jit(solution)/shard_map/all_to_all | solution.py:42
  93.6 65.8 %copy-start.3 = (f32[4,3,128]{2,0,1:T(4,128)}, f32[4,3,128]{2,0,1:T(4,128)S(1)}, u32[]{:S(2)}) copy-start(f32[4,3,128]{2,0,1:T(4,128)S(1)} %fusion.1) | copy-start | bytes 18436
